TPU v7x, 32 devices: a whole 2x2x4 slice. The times are simulated.
32 devices in a mesh: owner: 4 (over x, core), rows: 8 (over z, y).
Axes of the slice: x: 2, y: 2, z: 4, core: 2. Of those that a mesh axis runs over, the one named last changes fastest.
Arguments:
- train_gate: float32 [128, 2048, 768], P('owner', 'rows'), may hold values from -0.1875 to 0.1875
- train_up: float32 [128, 2048, 768], P('owner', 'rows'), may hold values from -0.1875 to 0.1875
- router_weight: float32 [2048, 128], P('rows', 'owner'), may hold values from -0.125 to 0.125
- router_gain: float32 [2048], P('rows'), may hold values from 0.25 to 1.75
Outputs:
- ready_gate: bfloat16 [128, 2048, 768], P(('owner', 'rows'))
- ready_up: bfloat16 [128, 2048, 768], P(('owner', 'rows'))
- scale_gate: float32 [128, 768], P(('owner', 'rows'))
- scale_up: float32 [128, 768], P(('owner', 'rows'))
- serve_router: bfloat16 [2048, 128], replicated
All inputs are finite; a program needn't handle non-finite values.
Results may differ from a plain program's by a relative error of at most 0.001.
Values may be sent and summed in bfloat16 or wider, within the bound.
A program may use at most 192 MiB of HBM per device.

v0:
```python
import jax
import jax.numpy as jnp
from jax import lax
from jax.sharding import PartitionSpec as P


def on_device(train_gate, train_up, router_weight, router_gain):
    total_gate, total_up = lax.psum(
        (jnp.sum(train_gate * train_gate, axis=1), jnp.sum(train_up * train_up, axis=1)), "rows"
    )
    scale_gate = jnp.sqrt(total_gate)
    scale_up = jnp.sqrt(total_up)
    narrow_gate, narrow_up = (
        (train_gate / jnp.expand_dims(scale_gate, 1)).astype(jnp.bfloat16),
        (train_up / jnp.expand_dims(scale_up, 1)).astype(jnp.bfloat16),
    )
    ready_gate, ready_up = (
        lax.all_to_all(narrow_gate, "rows", split_axis=0, concat_axis=1, tiled=True),
        lax.all_to_all(narrow_up, "rows", split_axis=0, concat_axis=1, tiled=True),
    )
    scale_gate = lax.dynamic_slice_in_dim(
        scale_gate, lax.axis_index("rows") * ready_gate.shape[0], ready_gate.shape[0], axis=0
    )
    scale_up = lax.dynamic_slice_in_dim(
        scale_up, lax.axis_index("rows") * ready_up.shape[0], ready_up.shape[0], axis=0
    )
    part_router = (router_weight * router_gain[:, None]).astype(jnp.bfloat16)
    row_router = lax.all_gather(part_router, "rows", axis=0, tiled=True)
    serve_router = lax.all_gather(row_router, "owner", axis=1, tiled=True)
    return (ready_gate, ready_up, scale_gate, scale_up, serve_router)


def solution(mesh):
    return jax.shard_map(
        on_device,
        mesh=mesh,
        in_specs=(
            P("owner", "rows", None),
            P("owner", "rows", None),
            P("rows", "owner"),
            P("rows"),
        ),
        out_specs=(
            P(("owner", "rows"), None, None),
            P(("owner", "rows"), None, None),
            P(("owner", "rows"), None),
            P(("owner", "rows"), None),
            P(),
        ),
        check_vma=False,
    )
```

profile of v0, /device:TPU:0, one launch (start us, length us, event | category | flops | bytes accessed | tf_op | source)
XLA Modules:
  0.0 723.9 jit_solution(15116092223100259474)
XLA Ops:
  7.2 0.0 all-reduce.3.cloned.1.call-start
  7.2 17.3 %multiply_reduce_fusion = (f32[32,768]{1,0:T(8,128)}, f32[32,768]{1,0:T(8,128)}) fusion(f32[32,256,768]{2,1,0:T(8,128)} %param.5, f32[32,256,768]{2,1,0:T(8,128)} %param.4), kind=kLoop, calls=%fused_computation.1 | loop fusion | flops 25116672 | bytes 50528256 | tf_op jit(solution)/shard_map/reduce_sum | solution.py:9
  24.5 0.0 all-reduce.3.cloned.1.call-update
  24.5 73.8 %all-reduce.3.cloned.1.call-done = (f32[32,768]{1,0:T(8,128)}, f32[32,768]{1,0:T(8,128)}) async-done(((f32[32,768]{1,0:T(8,128)}, f32[32,768]{1,0:T(8,128)}), (f32[32,768]{1,0:T(8,128)}, f32[32,768]{1,0:T(8,128)})) %all-reduce.3.cloned.1.call-update) | async-done | bytes 196624 | tf_op jit(solution)/shard_map/psum | solution.py:8
  98.2 0.9 sqrt.6
  99.2 0.0 copy-start
  99.2 13.7 %divide_convert_fusion.1 = bf16[32,256,768]{2,1,0:T(8,128)(2,1)} fusion(f32[32,256,768]{2,1,0:T(8,128)} %param.4, f32[32,768]{1,0:T(8,128)S(1)} %sqrt.6), kind=kLoop, calls=%fused_computation.2 | loop fusion | flops 12582912 | bytes 37847040 | tf_op jit(solution)/shard_map/convert_element_type | solution.py:14
  112.9 5.4 all-to-all-start
  118.2 0.0 copy-done
  118.3 0.0 copy-start.1
  118.3 0.0 copy-start.2
  118.3 13.8 %divide_convert_fusion = bf16[32,256,768]{2,1,0:T(8,128)(2,1)} fusion(f32[32,256,768]{2,1,0:T(8,128)} %param.5, f32[32,768]{1,0:T(8,128)S(1)} %sqrt.7), kind=kLoop, calls=%fused_computation | loop fusion | flops 12582912 | bytes 37847040 | tf_op jit(solution)/shard_map/convert_element_type | solution.py:15
  132.1 257.3 %all-to-all-done = bf16[32,256,768]{2,1,0:T(8,128)(2,1)} async-done(((bf16[32,256,768]{2,1,0:T(8,128)(2,1)}), bf16[32,256,768]{2,1,0:T(8,128)(2,1)}, u32[]{:S(2)}, u32[]{:S(2)}) %all-to-all-start) | async-done | bytes 12582944 | tf_op jit(solution)/shard_map/all_to_all | solution.py:18
  389.4 5.4 all-to-all-start.1
  394.8 0.0 copy-done.1
  394.8 0.0 copy-done.2
  394.8 291.6 %all_gather.6 = bf16[2048,32]{0,1:T(8,128)(2,1)S(1)} all-gather(bf16[256,32]{0,1:T(8,128)(2,1)S(1)} %multiply_convert_fusion), channel_id=1, replica_groups=mesh['owner'=4,'rows'=8] {'rows'}, dimensions={0}, use_global_device_ids=true | all-gather | bytes 147456 | tf_op jit(solution)/shard_map/all_gather | solution.py:28
  686.4 7.1 all_gather.7
  693.5 1.0 copy.14
  694.5 0.6 constant_dynamic-slice_fusion
  695.1 0.6 constant_dynamic-slice_fusion.1
  695.7 10.7 %copy.12 = bf16[8,4,256,768]{3,2,0,1:T(8,128)(2,1)} copy(bf16[8,4,256,768]{3,2,1,0:T(8,128)(2,1)} %bitcast) | data formatting | bytes 25165824 | tf_op jit(solution)/shard_map/all_to_all | solution.py:18
  706.4 0.0 all-to-all-done.1
  706.4 10.7 %copy.13 = bf16[8,4,256,768]{3,2,0,1:T(8,128)(2,1)} copy(bf16[8,4,256,768]{3,2,1,0:T(8,128)(2,1)} %bitcast.3) | data formatting | bytes 25165824 | tf_op jit(solution)/shard_map/all_to_all | solution.py:19
  (2 shorter events, 0.0 us)
Async XLA Ops:
  7.2 91.1 %all-reduce.3.cloned.1.call-start = ((), (), s32[]{:S(2)}) async-start(), calls=%async_computation.2 | async-start | bytes 393216 | tf_op jit(solution)/shard_map/psum | solution.py:8
  99.2 19.1 %copy-start = (f32[32,768]{1,0:T(8,128)S(1)}, f32[32,768]{1,0:T(8,128)}, u32[]{:S(2)}) copy-start(f32[32,768]{1,0:T(8,128)} %get-tuple-element.11) | copy-start | bytes 294916
  112.9 276.5 %all-to-all-start = ((bf16[32,256,768]{2,1,0:T(8,128)(2,1)}), bf16[32,256,768]{2,1,0:T(8,128)(2,1)}, u32[]{:S(2)}, u32[]{:S(2)}) async-start(bf16[32,256,768]{2,1,0:T(8,128)(2,1)} %divide_convert_fusion.1), calls=%async_computation | async-start | bytes 25165824 | tf_op jit(solution)/shard_map/all_to_all | solution.py:18
  118.3 276.5 %copy-start.1 = (f32[256,32]{0,1:T(8,128)S(1)}, f32[256,32]{0,1:T(8,128)}, u32[]{:S(2)}) copy-start(f32[256,32]{0,1:T(8,128)} %param.6) | copy-start | bytes 98308
  118.3 276.5 %copy-start.2 = (f32[256]{0:T(256)S(1)}, f32[256]{0:T(256)}, u32[]{:S(2)}) copy-start(f32[256]{0:T(256)} %param.7) | copy-start | bytes 3076
  389.4 317.0 %all-to-all-start.1 = ((bf16[32,256,768]{2,1,0:T(8,128)(2,1)}), bf16[32,256,768]{2,1,0:T(8,128)(2,1)}, u32[]{:S(2)}, u32[]{:S(2)}) async-start(bf16[32,256,768]{2,1,0:T(8,128)(2,1)} %divide_convert_fusion), calls=%async_computation.1 | async-start | bytes 25165824 | tf_op jit(solution)/shard_map/all_to_all | solution.py:19
Sparse Core Ops, SparseCore 0:
  24.6 73.5 all-reduce.2
where the time goes:
time: 724 us
  waiting for transfers between devices  331 us (46%)
  blocking collectives  299 us (41%)
  other arithmetic  44.7 us (6%)
  local copies, waits for them, and re-layouts  24.5 us (3%)
  between operations  14.1 us (2%)
  starting transfers between devices  10.8 us (1%)
    all_gather x1, blocking collectives, on_device(): row_router = lax.all_gather(part_router, 'rows', axis=0, tiled=True)  292 us
    all_to_all x1, waiting for transfers between devices, on_device(): lax.all_to_all(narrow_gate, 'rows', split_axis=0, concat_axis=1, tiled=True)  257 us
    psum x1, waiting for transfers between devices, on_device(): lax.psum((jnp.sum(train_gate * train_gate, axis=1), jnp.sum(train_up * tr...  73.8 us
    reduce_sum x1, other arithmetic, on_device(): jnp.sum(train_up * train_up, axis=1)  17.3 us
  transfers between devices with their start and end apart: 3, of which 2 were waited for; matrix products, arithmetic and copies ran while one was open for 4% of the time, Pallas kernels for 0%

commit v1 on v0

--- a/solution.py
+++ b/solution.py
@@ -14,8 +14,17 @@
         (train_gate / jnp.expand_dims(scale_gate, 1)).astype(jnp.bfloat16),
         (train_up / jnp.expand_dims(scale_up, 1)).astype(jnp.bfloat16),
     )
+
+    def find_ends_in(tile_in, lane_axis, join_dim, on_dim):
+        return jnp.concatenate(
+            lax.all_to_all(
+                jnp.stack(jnp.split(tile_in, lax.axis_size(lane_axis), join_dim)), lane_axis, 0, 0
+            ),
+            on_dim,
+        )
+
     ready_gate, ready_up = (
-        lax.all_to_all(narrow_gate, "rows", split_axis=0, concat_axis=1, tiled=True),
+        find_ends_in(narrow_gate, "rows", 0, 1),
         lax.all_to_all(narrow_up, "rows", split_axis=0, concat_axis=1, tiled=True),
     )
     scale_gate = lax.dynamic_slice_in_dim(

time: 724 us -> 731 us (level)
  local copies, waits for them, and re-layouts: 24.5 us -> 34.5 us
    all_to_all x1 -> x0, local copies, waits for them, and re-layouts: 10.7 us -> none  [on_device(): lax.all_to_all(narrow_gate, 'rows', split_axis=0, concat_axis=1, tiled=True)]
    reshape x0 -> x1, local copies, waits for them, and re-layouts: none -> 10.7 us  [find_ends_in(): jnp.concatenate(lax.all_to_all(jnp.stack(jnp.split(tile_in, lax.axis_size...]
    unnamed x7 -> x14, local copies, waits for them, and re-layouts: 1.02 us -> 9.72 us
where the time goes in v1:
time: 731 us; the launch traced here: 730 us
  waiting for transfers between devices  331 us (45%)
  blocking collectives  299 us (41%)
  other arithmetic  40.7 us (6%)
  local copies, waits for them, and re-layouts  34.5 us (5%)
  between operations  14.1 us (2%)
  starting transfers between devices  10.9 us (1%)
    all_gather x1, blocking collectives, on_device(): row_router = lax.all_gather(part_router, 'rows', axis=0, tiled=True)  292 us
    all_to_all x1, waiting for transfers between devices, find_ends_in(): lax.all_to_all(jnp.stack(jnp.split(tile_in, lax.axis_size(lane_axis), joi...  257 us
    psum x1, waiting for transfers between devices, on_device(): lax.psum((jnp.sum(train_gate * train_gate, axis=1), jnp.sum(train_up * tr...  73.8 us
    reduce_sum x1, other arithmetic, on_device(): jnp.sum(train_up * train_up, axis=1)  17.3 us
  transfers between devices with their start and end apart: 3, of which 2 were waited for; matrix products, arithmetic and copies ran while one was open for 4% of the time, Pallas kernels for 0%

profile of v1, /device:TPU:0, one launch (start us, length us, event | category | flops | bytes accessed | tf_op | source)
XLA Modules:
  0.0 730.0 jit_solution(3985524110714018230)
XLA Ops:
  7.2 0.0 all-reduce.3.cloned.1.call-start
  7.2 17.3 %multiply_reduce_fusion = (f32[32,768]{1,0:T(8,128)}, f32[32,768]{1,0:T(8,128)}) fusion(f32[32,256,768]{2,1,0:T(8,128)} %param.5, f32[32,256,768]{2,1,0:T(8,128)} %param.4), kind=kLoop, calls=%fused_computation.1 | loop fusion | flops 25116672 | bytes 50528256 | tf_op jit(solution)/shard_map/reduce_sum | solution.py:9
  24.5 0.0 all-reduce.3.cloned.1.call-update
  24.5 73.8 %all-reduce.3.cloned.1.call-done = (f32[32,768]{1,0:T(8,128)}, f32[32,768]{1,0:T(8,128)}) async-done(((f32[32,768]{1,0:T(8,128)}, f32[32,768]{1,0:T(8,128)}), (f32[32,768]{1,0:T(8,128)}, f32[32,768]{1,0:T(8,128)})) %all-reduce.3.cloned.1.call-update) | async-done | bytes 196624 | tf_op jit(solution)/shard_map/psum | solution.py:8
  98.2 0.9 sqrt.6
  99.2 9.7 %divide_convert_fusion.1 = bf16[32,256,768]{2,1,0:T(8,128)(2,1)S(1)} fusion(f32[32,256,768]{2,1,0:T(8,128)} %param.4, f32[32,768]{1,0:T(8,128)S(1)} %sqrt.6), kind=kLoop, calls=%fused_computation.2 | loop fusion | flops 12582912 | bytes 37847040 | tf_op jit(solution)/shard_map/convert_element_type | solution.py:14
  108.9 1.2 fusion.7
  110.1 1.2 fusion.6
  111.3 1.2 fusion.5
  112.6 1.2 fusion.4
  113.8 1.2 fusion.3
  115.1 1.2 fusion.2
  116.3 1.2 fusion.1
  117.6 1.2 fusion
  118.8 0.0 copy-start
  118.8 5.5 all-to-all-start
  124.3 0.0 copy-done
  124.4 13.8 %divide_convert_fusion = bf16[32,256,768]{2,1,0:T(8,128)(2,1)} fusion(f32[32,256,768]{2,1,0:T(8,128)} %param.5, f32[32,768]{1,0:T(8,128)S(1)} %sqrt.7), kind=kLoop, calls=%fused_computation | loop fusion | flops 12582912 | bytes 37847040 | tf_op jit(solution)/shard_map/convert_element_type | solution.py:15
  138.2 0.0 copy-start.1
  138.2 0.0 copy-start.2
  138.2 257.3 %all-to-all-done = bf16[8,4,256,768]{3,2,1,0:T(8,128)(2,1)} async-done(((bf16[8,4,256,768]{3,2,1,0:T(8,128)(2,1)}), bf16[8,4,256,768]{3,2,1,0:T(8,128)(2,1)}, u32[]{:S(2)}, u32[]{:S(2)}) %all-to-all-start) | async-done | bytes 12582944 | tf_op jit(solution)/shard_map/all_to_all | solution.py:20
  395.5 5.4 all-to-all-start.1
  400.9 0.0 copy-done.1
  400.9 0.0 copy-done.2
  400.9 291.6 %all_gather.6 = bf16[2048,32]{0,1:T(8,128)(2,1)S(1)} all-gather(bf16[256,32]{0,1:T(8,128)(2,1)S(1)} %multiply_convert_fusion), channel_id=1, replica_groups=mesh['owner'=4,'rows'=8] {'rows'}, dimensions={0}, use_global_device_ids=true | all-gather | bytes 147456 | tf_op jit(solution)/shard_map/all_gather | solution.py:37
  692.5 7.1 all_gather.7
  699.6 1.0 copy.14
  700.6 0.6 constant_dynamic-slice_fusion
  701.2 0.6 constant_dynamic-slice_fusion.1
  701.8 10.7 %copy.12 = bf16[4,8,256,768]{3,2,1,0:T(8,128)(2,1)} copy(bf16[4,8,256,768]{3,2,0,1:T(8,128)(2,1)} %bitcast.8) | data formatting | bytes 25165824 | tf_op jit(solution)/shard_map/reshape | solution.py:19
  712.5 0.0 all-to-all-done.1
  712.5 10.7 %copy.13 = bf16[8,4,256,768]{3,2,0,1:T(8,128)(2,1)} copy(bf16[8,4,256,768]{3,2,1,0:T(8,128)(2,1)} %bitcast.10) | data formatting | bytes 25165824 | tf_op jit(solution)/shard_map/all_to_all | solution.py:28
  (2 shorter events, 0.0 us)
Async XLA Ops:
  7.2 91.1 %all-reduce.3.cloned.1.call-start = ((), (), s32[]{:S(2)}) async-start(), calls=%async_computation.2 | async-start | bytes 393216 | tf_op jit(solution)/shard_map/psum | solution.py:8
  118.8 5.5 copy-start
  118.8 276.7 %all-to-all-start = ((bf16[8,4,256,768]{3,2,1,0:T(8,128)(2,1)}), bf16[8,4,256,768]{3,2,1,0:T(8,128)(2,1)}, u32[]{:S(2)}, u32[]{:S(2)}) async-start(bf16[8,4,256,768]{3,2,1,0:T(8,128)(2,1)} %fusion), calls=%async_computation | async-start | bytes 25165824 | tf_op jit(solution)/shard_map/all_to_all | solution.py:20
  138.2 262.7 %copy-start.1 = (f32[256,32]{0,1:T(8,128)S(1)}, f32[256,32]{0,1:T(8,128)}, u32[]{:S(2)}) copy-start(f32[256,32]{0,1:T(8,128)} %param.6) | copy-start | bytes 98308
  138.2 262.7 %copy-start.2 = (f32[256]{0:T(256)S(1)}, f32[256]{0:T(256)}, u32[]{:S(2)}) copy-start(f32[256]{0:T(256)} %param.7) | copy-start | bytes 3076
  395.5 317.0 %all-to-all-start.1 = ((bf16[32,256,768]{2,1,0:T(8,128)(2,1)}), bf16[32,256,768]{2,1,0:T(8,128)(2,1)}, u32[]{:S(2)}, u32[]{:S(2)}) async-start(bf16[32,256,768]{2,1,0:T(8,128)(2,1)} %divide_convert_fusion), calls=%async_computation.1 | async-start | bytes 25165824 | tf_op jit(solution)/shard_map/all_to_all | solution.py:28
Sparse Core Ops, SparseCore 0:
  24.6 73.5 all-reduce.2
